TPU v7x, 256 devices: a 8x8x2 block of a 8x8x16 slice. The times are simulated.
256 devices in a mesh: member: 2 (over z), lat: 16 (over x, core), lon: 8 (over y).
Axes of the slice: x: 8, y: 8, z: 2, core: 2. Of those that a mesh axis runs over, the one named last changes fastest.
The devices are a block of a 8x8x16 slice.
Arguments:
- field: bfloat16 [1024, 1024, 256], P(('member', 'lat'), 'lon'), parts along dimension 0, may hold values from -6 to 6
- mode_table: int32 [384], replicated, may hold values from 0 to 383, as said below
- analysis: bfloat16 [384, 384, 512], P(('lat', 'lon')), as said below
- synthesis: bfloat16 [384, 384, 512], P(('lat', 'lon')), as said below
- mixing: bfloat16 [1, 2, 256, 256], replicated, may hold values from -0.25 to 0.25
- degree_gain: float32 [1, 384, 256], replicated, may hold values from 0.25 to 1.75
- skip_weight: bfloat16 [1, 256, 256], replicated, may hold values from -0.375 to 0.375
Outputs:
- advanced: bfloat16 [1024, 1024, 256], P(('member', 'lat'), 'lon'), parts along dimension 0
- spectrum: bfloat16 [768, 384, 2, 256], P(('member', 'lat', 'lon')), parts along dimension 0
There are 2 independent parts, one for each index of `member`. A program takes and returns all parts, laid end to end along the dimension named above; an argument that names none is the same for every part. Nothing has to cross between parts.
Inputs may be any that keep to these rules, and one draw needn't show every extreme that they name: A permutation of 0 to 383; slot s of the spectral layout holds zonal wavenumber mode_table[s]. analysis[s, l, j] = weight[j] P(l, m, colat[j]) rounded to bfloat16, with m = mode_table[s], colat[j] = pi (j + 0.5) / 512, weight[j] = 2 pi^2 sin(colat[j]) / 524288, and P the orthonormal associated Legendre function of degree l and order m at cos(colat) without the Condon-Shortley phase, zero for l < m. synthesis[s, l, j] = c P(l, m, colat[j]) rounded to bfloat16, with m = mode_table[s], c = 1 where m = 0 and c = 2 elsewhere, P and colat as for analysis.
All inputs are finite; a program needn't handle non-finite values.
Results may differ from a plain program's by a relative error of at most 0.0062.
Values may be sent and summed in bfloat16 or wider, within the bound.
No kernel may reach another device: no remote copies, remote signals or barrier semaphores. Data moves between devices by JAX's collectives and lax.ppermute only.
A program may use at most 64 MiB of HBM per device.

v0:
```python
import math

import jax
import jax.numpy as jnp
from jax import lax
from jax.sharding import PartitionSpec as P


def split_up(value, dim, devices):
    dims = value.shape
    parts = value.reshape(*dims[:dim], devices, dims[dim] // devices, *dims[dim + 1 :])
    return jnp.moveaxis(parts, dim, 0)


def joined_along(parts, dim):
    dims = list(parts.shape[1:])
    dims[dim] *= parts.shape[0]
    return jnp.moveaxis(parts, 0, dim).reshape(dims)


def exchange_both(value, axis, axes, splits, concats):
    sizes = [lax.axis_size(a) for a in axes]
    parts = split_up(value, splits[0], sizes[0])
    parts = jnp.moveaxis(split_up(parts, splits[1] + 1, sizes[1]), 0, 1)
    inside = parts.shape[2:]
    parts = parts.reshape(-1, *inside)
    parts = lax.all_to_all(parts, axis, split_axis=0, concat_axis=0, tiled=True)
    parts = joined_along(parts.reshape(*sizes, *inside), concats[0] + 1)
    return joined_along(parts, concats[1])


def fourier_table(orders, length):
    phases = orders[:, None] * jnp.arange(length, dtype=jnp.int32)[None, :] % length
    angles = phases.astype(jnp.float32) * (2.0 * math.pi / length)
    return (
        jnp.stack([jnp.cos(angles), -jnp.sin(angles)], axis=1)
        .reshape(2 * orders.shape[0], length)
        .astype(jnp.bfloat16)
    )


def update(current, spectral, skip_matrix):
    shape_lead = current.shape
    direct = jnp.dot(
        current.reshape(-1, shape_lead[-1]), skip_matrix, preferred_element_type=jnp.float32
    ).reshape(shape_lead)
    pre_act = spectral.astype(jnp.float32) + direct
    return (current.astype(jnp.float32) + jax.nn.gelu(pre_act, approximate=False)).astype(
        jnp.bfloat16
    )


def per_device(field, mode_table, analysis, synthesis, mixing, degree_gain, skip_weight):
    lat_count = lax.axis_size("lat")
    lon_count = lax.axis_size("lon")
    lat_dev, lon_dev, channels = field.shape
    rows_full = lat_dev * lat_count
    points = lon_dev * lon_count
    mode_count = mode_table.shape[0]
    per_group = analysis.shape[0]
    row_band = lat_dev // lon_count
    forward = fourier_table(mode_table, points)
    analysis = analysis.reshape(per_group, mode_count, lat_count, lon_count, row_band)
    analysis = jnp.transpose(analysis, (0, 1, 3, 2, 4)).reshape(per_group, mode_count, rows_full)
    lon_ids = jnp.arange(lon_count, dtype=jnp.int32)[:, None, None]
    lat_ids = jnp.arange(lat_count, dtype=jnp.int32)[None, :, None]
    slot_ids = jnp.arange(per_group, dtype=jnp.int32)[None, None, :]
    slot_order = ((lat_ids * lon_count + lon_ids) * per_group + slot_ids).reshape(-1)
    backward = fourier_table(mode_table[slot_order], points)
    mixed_last = None
    current = field
    row_block = lax.all_to_all(current, "lon", split_axis=0, concat_axis=1, tiled=True)
    lat_side = jnp.einsum(
        "rkc,qk->rqc", row_block, forward, preferred_element_type=jnp.float32
    ).astype(jnp.bfloat16)
    gathered = exchange_both(lat_side, ("lat", "lon"), ("lat", "lon"), (1, 1), (0, 0))
    lat_data = gathered.reshape(rows_full, per_group, 2 * channels)
    coefficients = jnp.einsum(
        "slj,jsx->slx", analysis, lat_data, preferred_element_type=jnp.float32
    ).astype(jnp.bfloat16)
    real_part = mixing[0, 0]
    imag_part = mixing[0, 1]
    joined = jnp.concatenate(
        [
            jnp.concatenate([real_part, imag_part], axis=1),
            jnp.concatenate([-imag_part, real_part], axis=1),
        ],
        axis=0,
    )
    product = jnp.dot(
        coefficients.reshape(-1, 2 * channels), joined, preferred_element_type=jnp.float32
    )
    product = product.reshape(per_group, mode_count, 2, channels)
    mixed_modes = (product * degree_gain[0][None, :, None, :]).astype(jnp.bfloat16)
    synthesized = jnp.einsum(
        "slj,slx->jsx",
        synthesis,
        mixed_modes.reshape(per_group, mode_count, 2 * channels),
        preferred_element_type=jnp.float32,
    )
    synthesized = synthesized.astype(jnp.bfloat16).reshape(rows_full, 2 * per_group, channels)
    returned = exchange_both(synthesized, ("lat", "lon"), ("lat", "lon"), (0, 0), (1, 1))
    spectral = jnp.einsum(
        "rqc,qk->rkc", returned, backward, preferred_element_type=jnp.float32
    ).astype(jnp.bfloat16)
    spectral, mixed_last = (spectral, mixed_modes)
    grid_part = lax.all_to_all(spectral, "lon", split_axis=1, concat_axis=0, tiled=True)
    current = update(current, grid_part, skip_weight[0])
    return (current, mixed_last)


def solution(mesh):
    in_specs = (
        P(("member", "lat"), "lon", None),
        P(),
        P(("lat", "lon"), None, None),
        P(("lat", "lon"), None, None),
        P(),
        P(),
        P(),
    )
    out_specs = (P(("member", "lat"), "lon", None), P(("member", "lat", "lon"), None, None, None))
    return jax.shard_map(
        per_device, mesh=mesh, in_specs=in_specs, out_specs=out_specs, check_vma=False
    )
```

profile of v0, /device:TPU:640, one launch (start us, length us, event | category | flops | bytes accessed | tf_op | source)
XLA Modules:
  0.0 270.3 jit_solution(7713228131857832205)
XLA Ops:
  0.7 13.3 %all-to-all-start = ((bf16[32,128,256]{2,1,0:T(8,128)(2,1)}), bf16[32,128,256]{2,1,0:T(8,128)(2,1)S(1)}, u32[]{:S(2)}, u32[]{:S(2)}) async-start(bf16[32,128,256]{2,1,0:T(8,128)(2,1)} %param.7), calls=%async_computation | async-start | bytes 4194304 | tf_op jit(solution)/shard_map/all_to_all | solution.py:72
  14.0 7.0 %cosine_convert_fusion = (bf16[384,1,1024]{2,0,1:T(8,128)(2,1)S(1)}, bf16[384,1,1024]{2,0,1:T(8,128)(2,1)S(1)}) fusion(s32[384]{0:T(512)S(1)} %copy-done.2), kind=kLoop, calls=%fused_computation.47 | loop fusion | flops 6684672 | bytes 1574400 | tf_op jit(solution)/shard_map/convert.3
  21.1 2.8 %copy.133 = bf16[384,2,1024]{2,1,0:T(2,128)(2,1)} copy(bf16[384,2,1024]{2,0,1:T(8,128)(2,1)S(1)} %pad_maximum_fusion.1) | data formatting | bytes 3145728 | tf_op jit(solution)/shard_map/stack | solution.py:36
  23.9 3.7 %reshape.332 = bf16[768,1024,1]{1,0,2:T(8,128)(2,1)} reshape(bf16[384,2,1024]{2,1,0:T(2,128)(2,1)} %copy.133) | data formatting | bytes 3145728 | tf_op jit(solution)/shard_map/convert_element_type | solution.py:38
  27.5 37.7 %all-to-all-done = bf16[32,128,256]{2,1,0:T(8,128)(2,1)S(1)} async-done(((bf16[32,128,256]{2,1,0:T(8,128)(2,1)}), bf16[32,128,256]{2,1,0:T(8,128)(2,1)S(1)}, u32[]{:S(2)}, u32[]{:S(2)}) %all-to-all-start) | async-done | bytes 2097184 | tf_op jit(solution)/shard_map/all_to_all | solution.py:72
  65.4 1.3 copy-done.7
  66.6 1.8 convolution_convert_fusion.1
  69.9 2.4 copy.137
  72.3 13.4 %all-to-all-start.1 = ((bf16[128,4,6,256]{3,1,2,0:T(4,128)(2,1)}), bf16[128,4,6,256]{3,1,2,0:T(4,128)(2,1)S(1)}, u32[]{:S(2)}, u32[]{:S(2)}) async-start(bf16[128,4,6,256]{3,1,2,0:T(4,128)(2,1)} %copy.137), calls=%async_computation.1 | async-start | bytes 3145728 | tf_op jit(solution)/shard_map/all_to_all | solution.py:27
  86.8 2.4 copy.140
  89.1 3.3 %reshape.316 = bf16[3,384,16,8,4]{1,4,3,2,0:T(4,128)(2,1)} reshape(bf16[3,384,512]{1,2,0:T(8,128)(2,1)} %copy.140) | data formatting | bytes 2359296 | tf_op jit(solution)/shard_map/reshape | solution.py:63
  92.4 2.9 %copy.141 = bf16[3,384,8,16,4]{1,4,3,2,0:T(4,128)(2,1)} copy(bf16[3,384,8,16,4]{1,4,2,3,0:T(4,128)(2,1)} %bitcast.89) | data formatting | bytes 2359296 | tf_op jit(solution)/shard_map/transpose | solution.py:64
  95.3 3.2 %reshape.317 = bf16[3,384,512]{1,2,0:T(8,128)(2,1)} reshape(bf16[3,384,8,16,4]{1,4,3,2,0:T(4,128)(2,1)} %copy.141) | data formatting | bytes 2359296 | tf_op jit(solution)/shard_map/reshape | solution.py:64
  99.4 24.5 %all-to-all-done.1 = bf16[128,4,6,256]{3,1,2,0:T(4,128)(2,1)S(1)} async-done(((bf16[128,4,6,256]{3,1,2,0:T(4,128)(2,1)}), bf16[128,4,6,256]{3,1,2,0:T(4,128)(2,1)S(1)}, u32[]{:S(2)}, u32[]{:S(2)}) %all-to-all-start.1) | async-done | bytes 1572896 | tf_op jit(solution)/shard_map/all_to_all | solution.py:27
  125.2 2.7 %reshape_reshape_reshape.3 = bf16[512,3,512]{2,1,0:T(4,128)(2,1)} reshape(bf16[8,16,4,6,256]{4,3,2,1,0:T(8,128)(2,1)S(1)} %copy.139) | data formatting | bytes 3145728 | tf_op jit(solution)/shard_map/reshape;reshape;reshape | solution.py:77
  127.9 4.0 %multiply_convert_fusion = bf16[3,384,2,256]{1,3,2,0:T(8,128)(2,1)S(1)} fusion(bf16[2,256,512,1]{2,1,0,3:T(8,128)(2,1)} %bitcast.94, f32[384,256]{0,1:T(8,128)} %copy.146, bf16[3,384,512]{1,2,0:T(8,128)(2,1)} %reshape.317, bf16[512,3,512]{2,1,0:T(4,128)(2,1)} %reshape_reshape_reshape.3), kind=kOutput, calls=%fused_computation.28 | convolution fusion | flops 1209729024 | bytes 4849664 | tf_op jit(solution)/shard_map/dot_general | solution.py:90
  133.0 2.1 fusion.29
  135.1 3.2 %copy.147 = bf16[512,3,512]{2,1,0:T(4,128)(2,1)S(1)} copy(bf16[512,3,512]{0,2,1:T(8,128)(2,1)} %fusion.29) | data formatting | bytes 3145728 | tf_op jit(solution)/shard_map/convert_element_type | solution.py:101
  138.3 2.7 reshape_reshape_reshape_reshape.3
  141.0 3.4 %copy.148 = bf16[128,4,6,256]{3,1,2,0:T(4,128)(2,1)} copy(bf16[128,4,6,256]{3,2,1,0:T(8,128)(2,1)} %reshape_reshape_reshape_reshape.3) | data formatting | bytes 3145728 | tf_op jit(solution)/shard_map/reshape;reshape;reshape;reshape | solution.py:26
  144.4 11.2 %all-to-all-start.2 = ((bf16[128,4,6,256]{3,1,2,0:T(4,128)(2,1)}), bf16[128,4,6,256]{3,1,2,0:T(4,128)(2,1)S(1)}, u32[]{:S(2)}, u32[]{:S(2)}) async-start(bf16[128,4,6,256]{3,1,2,0:T(4,128)(2,1)} %copy.148), calls=%async_computation.2 | async-start | bytes 3145728 | tf_op jit(solution)/shard_map/all_to_all | solution.py:27
  155.9 2.8 %gather_fusion = s32[384]{0:T(512)S(1)} fusion(s32[384]{0:T(512)S(1)} %copy-done.2, s32[1024]{0:T(1024)S(1)} %pad_clamp_fusion), kind=kCustom, calls=%fused_computation | custom fusion | bytes 4608 | tf_op jit(solution)/shard_map/gather | solution.py:69
  158.7 7.0 %cosine_convert_fusion.1 = (bf16[384,1,1024]{2,0,1:T(8,128)(2,1)S(1)}, bf16[384,1,1024]{2,0,1:T(8,128)(2,1)S(1)}) fusion(s32[384]{0:T(512)S(1)} %gather_fusion), kind=kLoop, calls=%fused_computation.51 | loop fusion | flops 6684672 | bytes 1574400 | tf_op jit(solution)/shard_map/convert.5
  165.8 2.8 %copy.132 = bf16[384,2,1024]{2,1,0:T(2,128)(2,1)} copy(bf16[384,2,1024]{2,0,1:T(8,128)(2,1)S(1)} %pad_maximum_fusion) | data formatting | bytes 3145728 | tf_op jit(solution)/shard_map/stack | solution.py:36
  168.6 3.6 %convert_element_type.95 = bf16[768,1024]{1,0:T(8,128)(2,1)} reshape(bf16[384,2,1024]{2,1,0:T(2,128)(2,1)} %copy.132) | data formatting | bytes 3145728 | tf_op jit(solution)/shard_map/convert_element_type | solution.py:38
  172.2 21.5 %all-to-all-done.2 = bf16[128,4,6,256]{3,1,2,0:T(4,128)(2,1)S(1)} async-done(((bf16[128,4,6,256]{3,1,2,0:T(4,128)(2,1)}), bf16[128,4,6,256]{3,1,2,0:T(4,128)(2,1)S(1)}, u32[]{:S(2)}, u32[]{:S(2)}) %all-to-all-start.2) | async-done | bytes 1572896 | tf_op jit(solution)/shard_map/all_to_all | solution.py:27
  195.7 1.8 convert_bitcast_fusion
  197.5 2.9 %copy.153 = bf16[4,1024,256]{2,0,1:T(4,128)(2,1)} copy(bf16[4,1024,256]{2,1,0:T(8,128)(2,1)S(1)} %convert_bitcast_fusion) | data formatting | bytes 4194304 | tf_op jit(solution)/shard_map/convert_element_type | solution.py:105
  200.4 4.8 %all-to-all-start.3 = ((bf16[4,1024,256]{2,0,1:T(4,128)(2,1)}), bf16[4,1024,256]{2,0,1:T(4,128)(2,1)S(1)}, u32[]{:S(2)}, u32[]{:S(2)}) async-start(bf16[4,1024,256]{2,0,1:T(4,128)(2,1)} %copy.153), calls=%async_computation.3 | async-start | bytes 4194304 | tf_op jit(solution)/shard_map/all_to_all | solution.py:107
  205.2 2.8 %copy.155 = bf16[3,384,2,256]{3,2,1,0:T(2,128)(2,1)} copy(bf16[3,384,2,256]{1,3,2,0:T(8,128)(2,1)S(1)} %copy-done.4) | data formatting | bytes 2359296
  208.0 49.6 %all-to-all-done.3 = bf16[4,1024,256]{2,0,1:T(4,128)(2,1)S(1)} async-done(((bf16[4,1024,256]{2,0,1:T(4,128)(2,1)}), bf16[4,1024,256]{2,0,1:T(4,128)(2,1)S(1)}, u32[]{:S(2)}, u32[]{:S(2)}) %all-to-all-start.3) | async-done | bytes 2097184 | tf_op jit(solution)/shard_map/all_to_all | solution.py:107
  259.2 11.1 %fusion.3 = bf16[32,128,256]{2,1,0:T(8,128)(2,1)} fusion(bf16[32,128,256]{2,1,0:T(8,128)(2,1)S(1)} %copy-done.5, f32[4,8,128,256]{3,2,0,1:T(8,128)S(1)} %copy.154, bf16[1,256,256]{2,1,0:T(8,128)(2,1)S(1)} %copy-done.10), kind=kOutput, calls=%fused_computation.5 | convolution fusion | flops 608174080 | bytes 8519680 | tf_op jit(solution)/shard_map/dot_general | solution.py:44
  (43 shorter events, 10.0 us)
Async XLA Ops:
  0.6 132.3 %copy-start = (bf16[3,384,512]{2,1,0:T(8,128)(2,1)S(1)}, bf16[3,384,512]{2,1,0:T(8,128)(2,1)}, u32[]{:S(2)}) copy-start(bf16[3,384,512]{2,1,0:T(8,128)(2,1)} %param.10) | copy-start | bytes 3538948
  0.6 13.3 %copy-start.2 = (s32[384]{0:T(512)S(1)}, s32[384]{0:T(512)}, u32[]{:S(2)}) copy-start(s32[384]{0:T(512)} %param.8) | copy-start | bytes 4612
  0.7 64.6 %all-to-all-start = ((bf16[32,128,256]{2,1,0:T(8,128)(2,1)}), bf16[32,128,256]{2,1,0:T(8,128)(2,1)S(1)}, u32[]{:S(2)}, u32[]{:S(2)}) async-start(bf16[32,128,256]{2,1,0:T(8,128)(2,1)} %param.7), calls=%async_computation | async-start | bytes 4194304 | tf_op jit(solution)/shard_map/all_to_all | solution.py:72
  65.2 1.4 copy-start.7
  72.3 13.4 %copy-start.8 = (bf16[1,2,256,256]{3,2,1,0:T(8,128)(2,1)S(1)}, bf16[1,2,256,256]{3,2,1,0:T(8,128)(2,1)}, u32[]{:S(2)}) copy-start(bf16[1,2,256,256]{3,2,1,0:T(8,128)(2,1)} %param.11) | copy-start | bytes 786436
  72.3 51.7 %all-to-all-start.1 = ((bf16[128,4,6,256]{3,1,2,0:T(4,128)(2,1)}), bf16[128,4,6,256]{3,1,2,0:T(4,128)(2,1)S(1)}, u32[]{:S(2)}, u32[]{:S(2)}) async-start(bf16[128,4,6,256]{3,1,2,0:T(4,128)(2,1)} %copy.137), calls=%async_computation.1 | async-start | bytes 3145728 | tf_op jit(solution)/shard_map/all_to_all | solution.py:27
  92.4 6.1 %copy-start.9 = (f32[1,384,256]{2,1,0:T(8,128)S(1)}, f32[1,384,256]{2,1,0:T(8,128)}, u32[]{:S(2)}) copy-start(f32[1,384,256]{2,1,0:T(8,128)} %param.12) | copy-start | bytes 1179652
  131.9 1.0 copy-start.3
  144.4 49.4 %all-to-all-start.2 = ((bf16[128,4,6,256]{3,1,2,0:T(4,128)(2,1)}), bf16[128,4,6,256]{3,1,2,0:T(4,128)(2,1)S(1)}, u32[]{:S(2)}, u32[]{:S(2)}) async-start(bf16[128,4,6,256]{3,1,2,0:T(4,128)(2,1)} %copy.148), calls=%async_computation.2 | async-start | bytes 3145728 | tf_op jit(solution)/shard_map/all_to_all | solution.py:27
  194.2 1.4 copy-start.6
  200.4 4.8 %copy-start.4 = (bf16[3,384,2,256]{1,3,2,0:T(8,128)(2,1)S(1)}, bf16[3,384,2,256]{1,3,2,0:T(8,128)(2,1)}, u32[]{:S(2)}) copy-start(bf16[3,384,2,256]{1,3,2,0:T(8,128)(2,1)} %copy-done.3) | copy-start | bytes 3538948
  200.4 57.2 %all-to-all-start.3 = ((bf16[4,1024,256]{2,0,1:T(4,128)(2,1)}), bf16[4,1024,256]{2,0,1:T(4,128)(2,1)S(1)}, u32[]{:S(2)}, u32[]{:S(2)}) async-start(bf16[4,1024,256]{2,0,1:T(4,128)(2,1)} %copy.153), calls=%async_computation.3 | async-start | bytes 4194304 | tf_op jit(solution)/shard_map/all_to_all | solution.py:107
  257.6 1.6 copy-start.5
  257.6 1.6 copy-start.10
  259.2 11.1 %copy-start.1 = (bf16[3,384,512]{2,1,0:T(8,128)(2,1)S(1)}, bf16[3,384,512]{2,1,0:T(8,128)(2,1)}, u32[]{:S(2)}) copy-start(bf16[3,384,512]{2,1,0:T(8,128)(2,1)} %param.10) | copy-start | bytes 3538948
where the time goes:
time: 271 us; the launch traced here: 270 us
  waiting for transfers between devices  133 us (49%)
  local copies, waits for them, and re-layouts  58.2 us (21%)
  starting transfers between devices  42.6 us (16%)
  matrix products  20.8 us (8%)
  other arithmetic  14.4 us (5%)
    all_to_all x1, waiting for transfers between devices, per_device(): lax.all_to_all(spectral, 'lon', split_axis=1, concat_axis=0, tiled=True)  49.6 us
    all_to_all x2, waiting for transfers between devices, exchange_both(): parts = lax.all_to_all(parts, axis, split_axis=0, concat_axis=0, tiled=True)  46.1 us
    all_to_all x1, waiting for transfers between devices, per_device(): lax.all_to_all(current, 'lon', split_axis=0, concat_axis=1, tiled=True)  37.7 us
    all_to_all x2, starting transfers between devices, exchange_both(): parts = lax.all_to_all(parts, axis, split_axis=0, concat_axis=0, tiled=True)  24.5 us
    another operation x2, other arithmetic  13.9 us
    all_to_all x1, starting transfers between devices, per_device(): lax.all_to_all(current, 'lon', split_axis=0, concat_axis=1, tiled=True)  13.3 us
    dot_general x1, matrix products, update(): jnp.dot(current.reshape(-1, shape_lead[-1]), skip_matrix, preferred_eleme...  11.1 us
    unnamed x24, local copies, waits for them, and re-layouts  9.61 us
  transfers between devices with their start and end apart: 4, of which 4 were waited for; matrix products, arithmetic and copies ran while one was open for 17% of the time, Pallas kernels for 0%

commit v1 on v0

v1 whole, which is shorter than its diff:
```python
import math

import jax
import jax.numpy as jnp
from jax import lax
from jax.sharding import Mesh, PartitionSpec as P

SWAP = [(0, 1), (1, 0)]
OWNERS = ("latx", "lon")


def fourier_table(orders, length):
    phases = orders[:, None] * jnp.arange(length, dtype=jnp.int32)[None, :] % length
    angles = phases.astype(jnp.float32) * (2.0 * math.pi / length)
    return jnp.concatenate(
        [jnp.cos(angles).astype(jnp.bfloat16), (-jnp.sin(angles)).astype(jnp.bfloat16)], axis=0
    )


def update(current, spectral, skip_matrix):
    shape_lead = current.shape
    direct = jnp.dot(
        current.reshape(-1, shape_lead[-1]), skip_matrix, preferred_element_type=jnp.float32
    ).reshape(shape_lead)
    pre_act = spectral.astype(jnp.float32) + direct
    return (current.astype(jnp.float32) + jax.nn.gelu(pre_act, approximate=False)).astype(
        jnp.bfloat16
    )


def per_device(field, mode_table, analysis, synthesis, mixing, degree_gain, skip_weight):
    xs = lax.axis_size("latx")
    cores = lax.axis_size("core")
    lons = lax.axis_size("lon")
    core = lax.axis_index("core")
    lat_dev, lon_dev, channels = field.shape
    points = lon_dev * lons
    degrees = analysis.shape[1]
    slots = analysis.shape[0]
    band = lat_dev // lons
    rows_full = lat_dev * xs * cores
    owners = xs * lons
    bf16 = jnp.bfloat16
    f32 = jnp.float32

    rows = lax.all_to_all(field, "lon", split_axis=0, concat_axis=1, tiled=True)

    orders = mode_table.reshape(xs, cores, lons, slots)
    flip = core == 1
    own_orders = jnp.where(flip, orders[:, 1], orders[:, 0]).reshape(-1)
    far_orders = jnp.where(flip, orders[:, 0], orders[:, 1]).reshape(-1)
    far_table = fourier_table(far_orders, points)
    own_table = fourier_table(own_orders, points)

    place = jnp.arange(rows_full, dtype=jnp.int32)
    place_row = place % band
    place_core = (place // band) % cores
    place_lon = (place // (band * cores)) % lons
    place_x = place // (band * cores * lons)
    real_core = jnp.where(flip, 1 - place_core, place_core)
    real_row = ((place_x * cores + real_core) * lons + place_lon) * band + place_row
    pick = (jnp.arange(rows_full, dtype=jnp.int32)[:, None] == real_row[None, :]).astype(bf16)

    def picked(table):
        return jnp.dot(
            table.reshape(slots * degrees, rows_full), pick, preferred_element_type=f32
        ).astype(bf16).reshape(slots, degrees, rows_full)

    far_side = jnp.einsum("qk,rkc->qrc", far_table, rows, preferred_element_type=f32).astype(bf16)
    far_in = lax.ppermute(far_side, "core", SWAP)
    own_side = jnp.einsum("qk,rkc->qrc", own_table, rows, preferred_element_type=f32).astype(bf16)
    both = jnp.concatenate([own_side, far_in], axis=1)
    both = both.reshape(2, owners, slots, cores * band, channels)
    both = jnp.transpose(both, (1, 0, 2, 3, 4))
    gathered = lax.all_to_all(both, OWNERS, split_axis=0, concat_axis=0, tiled=True)
    lat_data = jnp.transpose(gathered, (1, 2, 0, 3, 4)).reshape(2, slots, rows_full, channels)

    forward = picked(analysis)
    backward = picked(synthesis)

    def degrees_of(part):
        return jnp.einsum("slj,sjc->slc", forward, part, preferred_element_type=f32).astype(bf16)

    def rows_of(part):
        return jnp.einsum("slj,slc->sjc", backward, part, preferred_element_type=f32).astype(bf16)

    def times(part, matrix):
        return jnp.einsum("slc,cd->sld", part, matrix, preferred_element_type=f32)

    coef_real = degrees_of(lat_data[0])
    coef_imag = degrees_of(lat_data[1])
    real_map = mixing[0, 0]
    imag_map = mixing[0, 1]
    gain = degree_gain[0][None]
    mixed_real = ((times(coef_real, real_map) - times(coef_imag, imag_map)) * gain).astype(bf16)
    mixed_imag = ((times(coef_real, imag_map) + times(coef_imag, real_map)) * gain).astype(bf16)
    mixed = jnp.stack([mixed_real, mixed_imag], axis=2)
    synthesized = jnp.stack([rows_of(mixed_real), rows_of(mixed_imag)], axis=0)
    synthesized = synthesized.reshape(2, slots, owners, cores * band, channels)
    synthesized = jnp.transpose(synthesized, (2, 0, 1, 3, 4))
    returned = lax.all_to_all(synthesized, OWNERS, split_axis=0, concat_axis=0, tiled=True)
    returned = jnp.transpose(returned, (1, 0, 2, 3, 4)).reshape(-1, cores * band, channels)
    far_back = lax.ppermute(returned[:, band:], "core", SWAP)
    own_back = returned[:, :band]
    spectral = jnp.einsum(
        "qrc,qk->rkc",
        jnp.concatenate([own_back, far_back], axis=0),
        jnp.concatenate([own_table, far_table], axis=0),
        preferred_element_type=f32,
    ).astype(bf16)
    spectral = jnp.transpose(spectral.reshape(band, lons, lon_dev, channels), (1, 0, 2, 3))
    grid_part = lax.all_to_all(spectral, "lon", split_axis=0, concat_axis=0, tiled=True)
    grid_part = grid_part.reshape(field.shape)
    return (update(field, grid_part, skip_weight[0]), mixed)


def solution(mesh):
    names = ("member", "latx", "core", "lon")
    sizes = dict(mesh.shape)
    chips = Mesh(
        mesh.devices.reshape(sizes["member"], sizes["lat"] // 2, 2, sizes["lon"]), names
    )
    in_specs = (
        P(("member", "latx", "core"), "lon", None),
        P(),
        P(("latx", "core", "lon"), None, None),
        P(("latx", "core", "lon"), None, None),
        P(),
        P(),
        P(),
    )
    out_specs = (
        P(("member", "latx", "core"), "lon", None),
        P(("member", "latx", "core", "lon"), None, None, None),
    )
    return jax.shard_map(
        per_device, mesh=chips, in_specs=in_specs, out_specs=out_specs, check_vma=False
    )
```

time: 271 us -> 254 us (0.937)
  blocking collectives: 0 us -> 49.6 us
  local copies, waits for them, and re-layouts: 58.2 us -> 12.7 us
  starting transfers between devices: 42.6 us -> 28.8 us
  other arithmetic: 14.4 us -> 8.14 us
  waiting for transfers between devices: 133 us -> 129 us
    all_to_all x0 -> x1, blocking collectives: none -> 49.6 us  [per_device(): lax.all_to_all(synthesized, OWNERS, split_axis=0, concat_axis=0, tiled=True)]
    another operation x6 -> x0, local copies, waits for them, and re-layouts: 15.2 us -> none  [the longest x2 6.03 us: exchange_both(): parts = parts.reshape(-1, *inside)]
    all_to_all x4 -> x3, starting transfers between devices: 42.6 us -> 28.5 us  [the longest x1 13.3 us: per_device(): rows = lax.all_to_all(field, 'lon', split_axis=0, concat_axis=1, tiled=True)]
    another operation x4 -> x1, other arithmetic: 14.2 us -> 0.11 us  [per_device(): mixed = jnp.stack([mixed_real, mixed_imag], axis=2)]
    convert_element_type x5 -> x2, local copies, waits for them, and re-layouts: 14 us -> 2.18 us  [picked(): return jnp.dot(table.reshape(slots * degrees, rows_full), pick, preferred...]
    all_to_all x4 -> x3, waiting for transfers between devices: 133 us -> 126 us  [the longest x1 49.2 us: per_device(): lax.all_to_all(spectral, 'lon', split_axis=0, concat_axis=0, tiled=True)]
    convert_element_type x0 -> x1, other arithmetic: none -> 7.75 us  [fourier_table(): jnp.cos(angles).astype(jnp.bfloat16)]
    reshape x4 -> x2, local copies, waits for them, and re-layouts: 9.34 us -> 1.74 us  [the longest x1 1.54 us: per_device(): spectral.reshape(band, lons, lon_dev, channels)]
  transfers between devices with their start and end apart: 4 -> 5, of which waited for: 4 -> 5; matrix products, arithmetic and copies ran while one was open for 17% -> 7% of each run, Pallas kernels for 0% -> 0%
where the time goes in v1:
time: 254 us; the launch traced here: 252 us
  waiting for transfers between devices  129 us (51%)
  blocking collectives  49.6 us (20%)
  starting transfers between devices  28.8 us (11%)
  matrix products  23.4 us (9%)
  local copies, waits for them, and re-layouts  12.7 us (5%)
  other arithmetic  8.14 us (3%)
    all_to_all x1, blocking collectives, per_device(): lax.all_to_all(synthesized, OWNERS, split_axis=0, concat_axis=0, tiled=True)  49.6 us
    all_to_all x1, waiting for transfers between devices, per_device(): lax.all_to_all(spectral, 'lon', split_axis=0, concat_axis=0, tiled=True)  49.2 us
    all_to_all x1, waiting for transfers between devices, per_device(): rows = lax.all_to_all(field, 'lon', split_axis=0, concat_axis=1, tiled=True)  43 us
    all_to_all x1, waiting for transfers between devices, per_device(): lax.all_to_all(both, OWNERS, split_axis=0, concat_axis=0, tiled=True)  33.3 us
    all_to_all x1, starting transfers between devices, per_device(): rows = lax.all_to_all(field, 'lon', split_axis=0, concat_axis=1, tiled=True)  13.3 us
    dot_general x1, matrix products, update(): jnp.dot(current.reshape(-1, shape_lead[-1]), skip_matrix, preferred_eleme...  12 us
    all_to_all x1, starting transfers between devices, per_device(): lax.all_to_all(both, OWNERS, split_axis=0, concat_axis=0, tiled=True)  10.2 us
    convert_element_type x1, other arithmetic, fourier_table(): jnp.cos(angles).astype(jnp.bfloat16)  7.75 us
  transfers between devices with their start and end apart: 5, of which 5 were waited for; matrix products, arithmetic and copies ran while one was open for 7% of the time, Pallas kernels for 0%

profile of v1, /device:TPU:640, one launch (start us, length us, event | category | flops | bytes accessed | tf_op | source)
XLA Modules:
  0.0 252.5 jit_solution(13908217108781348049)
XLA Ops:
  0.7 13.3 %all-to-all-start = ((bf16[32,128,256]{2,1,0:T(8,128)(2,1)}), bf16[32,128,256]{2,1,0:T(8,128)(2,1)S(1)}, u32[]{:S(2)}, u32[]{:S(2)}) async-start(bf16[32,128,256]{2,1,0:T(8,128)(2,1)} %param.7), calls=%async_computation | async-start | bytes 4194304 | tf_op jit(solution)/shard_map/all_to_all | solution.py:46
  14.5 7.8 %cosine_convert_fusion = (bf16[192,1024]{1,0:T(8,128)(2,1)}, bf16[192,1024]{1,0:T(8,128)(2,1)}, bf16[192,1024]{1,0:T(8,128)(2,1)}, bf16[192,1024]{1,0:T(8,128)(2,1)}) fusion(s32[192]{0:T(256)S(1)} %select_n.107, s32[192]{0:T(256)S(1)} %select_n.104), kind=kLoop, calls=%fused_computation.80 | loop fusion | flops 6684672 | bytes 1574400 | tf_op jit(solution)/shard_map/convert_element_type | solution.py:16
  22.2 43.0 %all-to-all-done = bf16[32,128,256]{2,1,0:T(8,128)(2,1)S(1)} async-done(((bf16[32,128,256]{2,1,0:T(8,128)(2,1)}), bf16[32,128,256]{2,1,0:T(8,128)(2,1)S(1)}, u32[]{:S(2)}, u32[]{:S(2)}) %all-to-all-start) | async-done | bytes 2097184 | tf_op jit(solution)/shard_map/all_to_all | solution.py:46
  65.4 0.9 copy-done.4
  66.3 1.0 convolution_convert_fusion.5
  67.5 1.0 convolution_convert_fusion.6
  68.5 1.2 collective-permute-done
  69.9 0.9 copy.38
  70.8 1.3 copy.39
  72.0 10.2 %all-to-all-start.1 = ((bf16[64,2,3,8,256]{4,3,2,1,0:T(8,128)(2,1)}), bf16[64,2,3,8,256]{4,3,2,1,0:T(8,128)(2,1)}, u32[]{:S(2)}, u32[]{:S(2)}) async-start(bf16[64,2,3,8,256]{4,3,2,1,0:T(8,128)(2,1)} %copy.39), calls=%async_computation.1 | async-start | bytes 3145728 | tf_op jit(solution)/shard_map/all_to_all | solution.py:75
  82.2 0.9 fusion.12
  83.1 0.6 copy.36
  83.8 3.2 %fusion.11 = bf16[1152,512]{0,1:T(8,128)(2,1)} fusion(bf16[1152,512]{1,0:T(8,128)(2,1)} %bitcast.103, s32[512]{0:T(512)S(1)} %fusion.71), kind=kOutput, calls=%fused_computation.23 | convolution fusion | flops 605093888 | bytes 2361344 | tf_op jit(solution)/shard_map/dot_general | solution.py:65
  87.0 1.6 copy.35
  88.5 33.3 %all-to-all-done.1 = bf16[64,2,3,8,256]{4,3,2,1,0:T(8,128)(2,1)} async-done(((bf16[64,2,3,8,256]{4,3,2,1,0:T(8,128)(2,1)}), bf16[64,2,3,8,256]{4,3,2,1,0:T(8,128)(2,1)}, u32[]{:S(2)}, u32[]{:S(2)}) %all-to-all-start.1) | async-done | bytes 1572896 | tf_op jit(solution)/shard_map/all_to_all | solution.py:75
  121.8 1.5 fusion.84
  123.3 0.5 convolution_convert_fusion.8
  123.8 0.5 copy-done.3
  124.9 0.5 convolution_convert_fusion.7
  125.6 0.3 fusion.24
  125.9 0.3 fusion.25
  126.3 0.6 fusion.26
  126.9 0.7 fusion.27
  127.7 49.6 %all_to_all.33 = bf16[64,2,3,8,256]{4,3,2,1,0:T(8,128)(2,1)S(1)} all-to-all(bf16[64,2,3,8,256]{4,3,2,1,0:T(8,128)(2,1)S(1)} %copy_bitcast_fusion.1), channel_id=1, replica_groups=mesh['member'=2,'latx'=8,'core'=2,'lon'=8] {'latx','lon'}, dimensions={0} | all-to-all | bytes 3145728 | tf_op jit(solution)/shard_map/all_to_all | solution.py:101
  177.4 0.5 fusion.83
  178.3 2.1 collective-permute-done.1
  180.5 1.9 convolution_convert_fusion.2
  182.3 1.5 copy.69
  183.9 5.0 %all-to-all-start.3 = ((bf16[8,4,128,256]{3,2,1,0:T(8,128)(2,1)}), bf16[8,4,128,256]{3,2,1,0:T(8,128)(2,1)}, u32[]{:S(2)}, u32[]{:S(2)}) async-start(bf16[8,4,128,256]{3,2,1,0:T(8,128)(2,1)} %bitcast.87), calls=%async_computation.3 | async-start | bytes 4194304 | tf_op jit(solution)/shard_map/all_to_all | solution.py:112
  189.0 2.2 copy.51
  191.2 49.2 %all-to-all-done.3 = bf16[8,4,128,256]{3,2,1,0:T(8,128)(2,1)} async-done(((bf16[8,4,128,256]{3,2,1,0:T(8,128)(2,1)}), bf16[8,4,128,256]{3,2,1,0:T(8,128)(2,1)}, u32[]{:S(2)}, u32[]{:S(2)}) %all-to-all-start.3) | async-done | bytes 2097184 | tf_op jit(solution)/shard_map/all_to_all | solution.py:112
  240.5 12.0 %fusion.3 = bf16[32,128,256]{2,1,0:T(8,128)(2,1)} fusion(bf16[32,128,256]{2,1,0:T(8,128)(2,1)S(1)} %copy-done.1, bf16[32,128,256]{2,1,0:T(8,128)(2,1)} %bitcast.41, bf16[1,256,256]{2,1,0:T(8,128)(2,1)S(1)} %copy-done.13), kind=kOutput, calls=%fused_computation.4 | convolution fusion | flops 609222656 | bytes 6422528 | tf_op jit(solution)/shard_map/dot_general | solution.py:22
  (42 shorter events, 2.6 us)
Async XLA Ops:
  0.6 81.6 %copy-start = (bf16[3,384,512]{2,1,0:T(8,128)(2,1)S(1)}, bf16[3,384,512]{2,1,0:T(8,128)(2,1)}, u32[]{:S(2)}) copy-start(bf16[3,384,512]{2,1,0:T(8,128)(2,1)} %param.9) | copy-start | bytes 3538948
  0.6 13.3 %copy-start.12 = (s32[384]{0:T(512)S(1)}, s32[384]{0:T(512)}, u32[]{:S(2)}) copy-start(s32[384]{0:T(512)} %param.8) | copy-start | bytes 4612
  0.7 64.6 %all-to-all-start = ((bf16[32,128,256]{2,1,0:T(8,128)(2,1)}), bf16[32,128,256]{2,1,0:T(8,128)(2,1)S(1)}, u32[]{:S(2)}, u32[]{:S(2)}) async-start(bf16[32,128,256]{2,1,0:T(8,128)(2,1)} %param.7), calls=%async_computation | async-start | bytes 4194304 | tf_op jit(solution)/shard_map/all_to_all | solution.py:46
  65.2 1.0 copy-start.4
  65.2 1.1 copy-start.6
  66.3 1.1 copy-start.8
  66.3 1.2 copy-start.10
  67.3 2.4 collective-permute-start
  72.0 49.8 %all-to-all-start.1 = ((bf16[64,2,3,8,256]{4,3,2,1,0:T(8,128)(2,1)}), bf16[64,2,3,8,256]{4,3,2,1,0:T(8,128)(2,1)}, u32[]{:S(2)}, u32[]{:S(2)}) async-start(bf16[64,2,3,8,256]{4,3,2,1,0:T(8,128)(2,1)} %copy.39), calls=%async_computation.1 | async-start | bytes 3145728 | tf_op jit(solution)/shard_map/all_to_all | solution.py:75
  123.3 1.0 copy-start.3
  124.6 1.0 copy-start.2
  177.9 2.6 %copy-start.5 = (bf16[192,1024]{1,0:T(8,128)(2,1)S(1)}, bf16[192,1024]{1,0:T(8,128)(2,1)}, u32[]{:S(2)}) copy-start(bf16[192,1024]{1,0:T(8,128)(2,1)} %get-tuple-element.16) | copy-start | bytes 1179652
  177.9 2.6 %copy-start.7 = (bf16[192,1024]{1,0:T(8,128)(2,1)S(1)}, bf16[192,1024]{1,0:T(8,128)(2,1)}, u32[]{:S(2)}) copy-start(bf16[192,1024]{1,0:T(8,128)(2,1)} %get-tuple-element.17) | copy-start | bytes 1179652
  177.9 2.5 %copy-start.9 = (bf16[192,1024]{1,0:T(8,128)(2,1)S(1)}, bf16[192,1024]{1,0:T(8,128)(2,1)}, u32[]{:S(2)}) copy-start(bf16[192,1024]{1,0:T(8,128)(2,1)} %get-tuple-element.18) | copy-start | bytes 1179652
  177.9 2.5 %copy-start.11 = (bf16[192,1024]{1,0:T(8,128)(2,1)S(1)}, bf16[192,1024]{1,0:T(8,128)(2,1)}, u32[]{:S(2)}) copy-start(bf16[192,1024]{1,0:T(8,128)(2,1)} %get-tuple-element.19) | copy-start | bytes 1179652
  178.0 2.4 collective-permute-start.1
  183.9 56.6 %all-to-all-start.3 = ((bf16[8,4,128,256]{3,2,1,0:T(8,128)(2,1)}), bf16[8,4,128,256]{3,2,1,0:T(8,128)(2,1)}, u32[]{:S(2)}, u32[]{:S(2)}) async-start(bf16[8,4,128,256]{3,2,1,0:T(8,128)(2,1)} %bitcast.87), calls=%async_computation.3 | async-start | bytes 4194304 | tf_op jit(solution)/shard_map/all_to_all | solution.py:112
  188.9 51.6 %copy-start.13 = (bf16[1,256,256]{2,1,0:T(8,128)(2,1)S(1)}, bf16[1,256,256]{2,1,0:T(8,128)(2,1)}, u32[]{:S(2)}) copy-start(bf16[1,256,256]{2,1,0:T(8,128)(2,1)} %param.13) | copy-start | bytes 393220
  189.0 51.5 %copy-start.1 = (bf16[32,128,256]{2,1,0:T(8,128)(2,1)S(1)}, bf16[32,128,256]{2,1,0:T(8,128)(2,1)}, u32[]{:S(2)}) copy-start(bf16[32,128,256]{2,1,0:T(8,128)(2,1)} %param.7) | copy-start | bytes 6291460
